TPU v7x, 32 devices: a whole 2x2x4 slice. The times are simulated.
32 devices in a mesh: frame: 8 (over z, core), mp: 2 (over x), dp: 2 (over y).
Axes of the slice: x: 2, y: 2, z: 4, core: 2. Of those that a mesh axis runs over, the one named last changes fastest.
Arguments:
- tokens: bfloat16 [4, 8, 160, 5120], P('dp', 'frame', None, 'mp'), may hold values from -30 to 30
- token_mask: int32 [4, 8, 160], P('dp', 'frame'), may hold values 0 or 1
- mask_embed: bfloat16 [5120], P('mp'), may hold values from -6 to 6
- w_qkv: bfloat16 [5120, 3, 3072], P('frame', None, 'mp'), may hold values from -0.078125 to 0.078125
- w_out: bfloat16 [3072, 5120], P('mp'), may hold values from -0.109375 to 0.109375
- action_idx: int32 [4, 8], P('dp', 'frame'), may hold values from 0 to 7
- codebook: float32 [8, 32], replicated, may hold values from -6 to 6
- act_proj: float32 [32, 5120], P(None, 'mp'), may hold values from -1 to 1
- cotangent: bfloat16 [4, 8, 160, 5120], P('dp', 'frame', None, 'mp'), may hold values from -6 to 6
Outputs:
- next_state: bfloat16 [4, 8, 160, 5120], P('dp', 'frame', None, 'mp')
- grad_proj: float32 [32, 5120], P(None, 'mp')
All inputs are finite; a program needn't handle non-finite values. No bound on the sum of `token_mask` on one device may be relied on, other than what follows from the above.
Results may differ from a plain program's by a relative error of at most 0.0098.
Values may be sent and summed in bfloat16 or wider, within the bound.
A program may use at most 128 MiB of HBM per device.

v0:
```python
import math

import jax
import jax.numpy as jnp
from jax import lax
from jax.sharding import PartitionSpec as P

HS = 128


floor_score = -1e30


def block_stats(query, past_keys, past_values, valid):
    scale = 1.0 / math.sqrt(HS)
    scores = (
        jnp.einsum("cphd,cnphd->cphn", query, past_keys, preferred_element_type=jnp.float32) * scale
    )
    scores = jnp.where(valid[None, None, None, :], scores, floor_score)
    peak = jnp.max(scores, axis=-1)
    weights = jnp.where(valid[None, None, None, :], jnp.exp(scores - peak[..., None]), 0.0)
    total = jnp.sum(weights, axis=-1)
    accum = jnp.einsum(
        "cphn,cnphd->cphd",
        weights,
        past_values.astype(jnp.float32),
        precision=lax.Precision.HIGHEST,
    )
    return (peak, total, accum)


def merge_stats(first, second):
    peak = jnp.maximum(first[0], second[0])
    right = jnp.exp(second[0] - peak)
    total = second[1] * right
    accum = second[2] * right[..., None]
    return (peak, total, accum)


def body(tokens, token_mask, mask_embed, w_qkv, w_out, action_idx, codebook, act_proj, cotangent):
    clip_count, _, spot_count, width_local = tokens.shape
    heads_width = w_qkv.shape[2]
    head_count = heads_width // HS
    xin = jnp.where(token_mask[..., None] == 1, mask_embed, tokens)
    row_block = xin.reshape(clip_count * spot_count, width_local)
    features = lax.all_gather(row_block, "mp", axis=1, tiled=True)
    piece = lax.all_gather(w_qkv, "frame", axis=0, tiled=True)
    count = piece.shape[0]
    qkv = jnp.dot(
        features, piece.reshape(count, 3 * heads_width), preferred_element_type=jnp.float32
    ).astype(jnp.bfloat16)
    query = qkv[:, :heads_width].reshape(clip_count, spot_count, head_count, HS)
    own_keys = qkv[:, heads_width : 2 * heads_width].reshape(clip_count, 1, spot_count, heads_width)
    own_values = qkv[:, 2 * heads_width :].reshape(clip_count, 1, spot_count, heads_width)
    own_frame = lax.axis_index("frame")
    start_carry = (
        jnp.full((clip_count, spot_count, head_count), floor_score, jnp.float32),
        jnp.zeros((clip_count, spot_count, head_count), jnp.float32),
        jnp.zeros((clip_count, spot_count, head_count, HS), jnp.float32),
    )
    piece_keys = lax.all_gather(own_keys, "frame", axis=1, tiled=True)
    piece_values = lax.all_gather(own_values, "frame", axis=1, tiled=True)
    count = piece_keys.shape[1]
    frame_ids = jnp.arange(count)
    stats = block_stats(
        query,
        piece_keys.reshape(clip_count, count, spot_count, head_count, HS),
        piece_values.reshape(clip_count, count, spot_count, head_count, HS),
        frame_ids <= own_frame,
    )
    peak, total, accum = merge_stats(start_carry, stats)
    attn = (
        (accum / total[..., None])
        .astype(jnp.bfloat16)
        .reshape(clip_count * spot_count, heads_width)
    )
    all_heads = lax.all_gather(attn, "mp", axis=1, tiled=True)
    out_block = lax.all_to_all(w_out, "mp", split_axis=1, concat_axis=0, tiled=True)
    mixed_rows = jnp.dot(all_heads, out_block, preferred_element_type=jnp.float32)
    mixed = mixed_rows.reshape(clip_count, 1, spot_count, width_local)
    onehot = (
        action_idx.reshape(clip_count)[:, None] == jnp.arange(codebook.shape[0])[None, :]
    ).astype(jnp.float32)
    codevec = jnp.dot(onehot, codebook, precision=lax.Precision.HIGHEST)
    gate = jnp.dot(codevec, act_proj, precision=lax.Precision.HIGHEST)
    next_state = (xin.astype(jnp.float32) + gate[:, None, None, :] * mixed).astype(jnp.bfloat16)
    dgate = jnp.sum(cotangent.astype(jnp.float32) * mixed, axis=2).reshape(clip_count, width_local)
    grad_terms = jnp.dot(codevec.T, dgate, precision=lax.Precision.HIGHEST)
    grad_proj = lax.psum(grad_terms, ("frame", "dp"))
    return (next_state, grad_proj)


def solution(mesh):
    in_specs = (
        P("dp", "frame", None, "mp"),
        P("dp", "frame", None),
        P("mp"),
        P("frame", None, "mp"),
        P("mp", None),
        P("dp", "frame"),
        P(),
        P(None, "mp"),
        P("dp", "frame", None, "mp"),
    )
    out_specs = (P("dp", "frame", None, "mp"), P(None, "mp"))
    return jax.shard_map(body, mesh=mesh, in_specs=in_specs, out_specs=out_specs, check_vma=False)
```

profile of v0, /device:TPU:1, one launch (start us, length us, event | category | flops | bytes accessed | tf_op | source)
XLA Modules:
  0.0 824.6 jit_solution(1975657170938718803)
XLA Ops:
  7.2 0.0 copy-start
  7.2 0.0 all-gather.6.cloned.1.call-start
  7.2 0.7 broadcast_compare_fusion
  8.0 2.8 broadcast_select_fusion
  10.7 0.0 all-gather.6.cloned.1.call-update
  10.8 0.0 all-gather.8.cloned.1.call-start
  10.8 8.8 %copy.25 = bf16[640,3,1536]{0,2,1:T(8,128)(2,1)} copy(bf16[640,3,1536]{2,0,1:T(8,128)(2,1)} %param.12) | data formatting | bytes 11796480 | tf_op args[3]
  19.7 0.0 all-gather.8.cloned.1.call-update
  19.7 0.0 all-gather.10.cloned.1.call-start
  19.7 39.5 %all-gather.6.cloned.1.call-done = bf16[320,5120]{1,0:T(8,128)(2,1)} async-done(((bf16[320,2560]{1,0:T(8,128)(2,1)}), bf16[320,5120]{1,0:T(8,128)(2,1)}) %all-gather.6.cloned.1.call-update) | async-done | bytes 3276816 | tf_op jit(solution)/shard_map/all_gather | solution.py:46
  59.2 403.8 %all-gather.8.cloned.1.call-done = bf16[5120,3,1536]{0,2,1:T(8,128)(2,1)} async-done(((bf16[640,3,1536]{0,2,1:T(8,128)(2,1)}), bf16[5120,3,1536]{0,2,1:T(8,128)(2,1)}) %all-gather.8.cloned.1.call-update) | async-done | bytes 47185936 | tf_op jit(solution)/shard_map/all_gather | solution.py:47
  463.0 24.1 %convolution_convert_fusion = bf16[320,4608]{1,0:T(8,128)(2,1)} fusion(bf16[320,5120]{1,0:T(8,128)(2,1)} %all-gather.6.cloned.1.call-done, bf16[5120,4608]{0,1:T(8,128)(2,1)} %bitcast.69), kind=kOutput, calls=%fused_computation.4 | convolution fusion | flops 15100968960 | bytes 53411840 | tf_op jit(solution)/shard_map/dot_general | solution.py:49
  487.1 3.3 fusion.16
  490.4 0.0 all-gather.10.cloned.1.call-update
  490.4 0.0 all-gather.12.cloned.1.call-start
  490.5 0.5 all-gather.12.cloned.1.call-update
  491.0 20.7 %copy.30 = bf16[1536,5120]{0,1:T(8,128)(2,1)} copy(bf16[1536,5120]{1,0:T(8,128)(2,1)} %param.13) | data formatting | bytes 31457280 | tf_op args[4]
  511.7 9.3 %all-to-all-start = ((bf16[1536,2,2560]{0,2,1:T(8,128)(2,1)}), bf16[1536,2,2560]{0,2,1:T(8,128)(2,1)}, u32[]{:S(2)}, u32[]{:S(2)}) async-start(bf16[1536,2,2560]{0,2,1:T(8,128)(2,1)} %bitcast.59), calls=%async_computation | async-start | bytes 31457280 | tf_op jit(solution)/shard_map/all_to_all | solution.py:78
  521.1 0.2 all-gather.14.cloned.1.call-start
  521.3 0.6 reshape.92
  521.9 44.6 %all-gather.10.cloned.1.call-done = bf16[2,8,160,1536]{3,2,1,0:T(8,128)(2,1)} async-done(((bf16[2,1,160,1536]{3,2,1,0:T(8,128)(2,1)}), bf16[2,8,160,1536]{3,2,1,0:T(8,128)(2,1)}) %all-gather.10.cloned.1.call-update) | async-done | bytes 7864336 | tf_op jit(solution)/shard_map/all_gather | solution.py:61
  566.5 15.2 %reshape.82 = bf16[2,8,160,12,128]{4,3,2,1,0:T(8,128)(2,1)} reshape(bf16[2,8,160,1536]{3,2,1,0:T(8,128)(2,1)} %all-gather.10.cloned.1.call-done) | data formatting | bytes 15728640 | tf_op jit(solution)/shard_map/reshape | solution.py:67
  581.7 10.6 %fusion.2 = f32[2,160,12,1,8]{4,3,2,1,0:T(1,128)} fusion(bf16[2,160,12,128,1]{3,4,2,1,0:T(2,128)(2,1)S(1)} %reshape.92, bf16[2,8,160,12,128]{4,3,2,1,0:T(8,128)(2,1)} %reshape.82), kind=kOutput, calls=%fused_computation.2 | convolution fusion | flops 7864320 | bytes 8970240 | tf_op jit(solution)/shard_map/cphd,cnphd->cphn/dot_general | solution.py:17
  592.3 3.6 copy.36
  595.9 0.1 fusion.7
  596.1 0.2 fusion.8
  596.2 0.1 copy.28
  596.4 0.1 copy.29
  596.5 1.3 copy.37
  597.8 47.0 %all-gather.12.cloned.1.call-done = bf16[2,8,160,1536]{3,2,1,0:T(8,128)(2,1)} async-done(((bf16[2,1,160,1536]{3,2,1,0:T(8,128)(2,1)}), bf16[2,8,160,1536]{3,2,1,0:T(8,128)(2,1)}) %all-gather.12.cloned.1.call-update) | async-done | bytes 7864336 | tf_op jit(solution)/shard_map/all_gather | solution.py:62
  644.8 15.1 %reshape.84 = bf16[2,8,160,12,128]{4,3,2,1,0:T(8,128)(2,1)} reshape(bf16[2,8,160,1536]{3,2,1,0:T(8,128)(2,1)} %all-gather.12.cloned.1.call-done) | data formatting | bytes 15728640 | tf_op jit(solution)/shard_map/reshape | solution.py:68
  659.9 17.1 %fusion = f32[2,160,12,1,128]{4,3,2,1,0:T(1,128)S(1)} fusion(f32[2,160,12,8,1]{3,4,2,1,0:T(1,128)S(1)} %copy.37, bf16[2,8,160,12,128]{4,3,2,1,0:T(8,128)(2,1)} %reshape.84), kind=kOutput, calls=%fused_computation | convolution fusion | flops 47185920 | bytes 9953280 | tf_op jit(solution)/shard_map/cphn,cnphd->cphd/dot_general | solution.py:23
  677.0 0.0 copy-start.4
  677.0 0.0 copy-start.5
  677.0 1.7 fusion.5
  678.8 1.2 copy.49
  680.0 0.0 all-gather.14.cloned.1.call-update
  680.0 0.3 all-reduce.2.cloned.1.call-start
  680.2 0.0 copy-done.4
  680.3 0.0 copy-done.5
  680.3 0.2 fusion.11
  680.5 0.0 copy-done
  680.5 0.3 fusion.17
  680.7 14.7 %all-to-all-done = bf16[1536,2,2560]{0,2,1:T(8,128)(2,1)} async-done(((bf16[1536,2,2560]{0,2,1:T(8,128)(2,1)}), bf16[1536,2,2560]{0,2,1:T(8,128)(2,1)}, u32[]{:S(2)}, u32[]{:S(2)}) %all-to-all-start) | async-done | bytes 15728672 | tf_op jit(solution)/shard_map/all_to_all | solution.py:78
  695.5 19.3 %copy.31 = bf16[2,1536,2560]{2,1,0:T(8,128)(2,1)} copy(bf16[2,1536,2560]{1,2,0:T(8,128)(2,1)} %bitcast.11) | data formatting | bytes 31457280 | tf_op jit(solution)/shard_map/all_to_all | solution.py:78
  714.8 0.0 all-gather.14.cloned.1.call-done
  714.8 0.0 copy-start.1
  714.8 0.0 copy-start.2
  714.8 0.0 copy-start.3
  714.8 9.4 %fusion.18 = f32[320,2560]{1,0:T(8,128)S(1)} fusion(bf16[320,3072]{1,0:T(8,128)(2,1)} %all-gather.14.cloned.1.call-done, bf16[3072,2560]{1,0:T(8,128)(2,1)} %bitcast.60), kind=kOutput, calls=%fused_computation.30 | convolution fusion | flops 5033164800 | bytes 20971520 | tf_op jit(solution)/shard_map/dot_general | solution.py:79
  724.2 0.0 copy-done.1
  724.2 0.0 copy-done.2
  724.2 0.0 copy-done.3
  724.2 2.1 multiply_reduce_fusion
  726.3 1.2 fusion.19
  727.5 0.0 all-reduce.2.cloned.1.call-update
  727.6 88.5 %all-reduce.2.cloned.1.call-done = f32[32,2560]{1,0:T(8,128)} async-done(((f32[32,2560]{1,0:T(8,128)}), f32[32,2560]{1,0:T(8,128)}) %all-reduce.2.cloned.1.call-update) | async-done | bytes 327696 | tf_op jit(solution)/shard_map/psum | solution.py:89
  816.1 1.7 copy.52
  (3 shorter events, 0.0 us)
Async XLA Ops:
  7.2 673.3 %copy-start = (f32[32,2560]{1,0:T(8,128)S(1)}, f32[32,2560]{1,0:T(8,128)}, u32[]{:S(2)}) copy-start(f32[32,2560]{1,0:T(8,128)} %param.16) | copy-start | bytes 983044
  7.2 52.0 %all-gather.6.cloned.1.call-start = ((), (), s32[]{:S(2)}) async-start(), calls=%async_computation.1 | async-start | bytes 4915200 | tf_op jit(solution)/shard_map/all_gather | solution.py:46
  10.8 452.2 %all-gather.8.cloned.1.call-start = ((), (), s32[]{:S(2)}) async-start(), calls=%async_computation.2 | async-start | bytes 53084160 | tf_op jit(solution)/shard_map/all_gather | solution.py:47
  19.7 546.8 %all-gather.10.cloned.1.call-start = ((), (), s32[]{:S(2)}) async-start(), calls=%async_computation.3 | async-start | bytes 8847360 | tf_op jit(solution)/shard_map/all_gather | solution.py:61
  490.4 154.4 %all-gather.12.cloned.1.call-start = ((), (), s32[]{:S(2)}) async-start(), calls=%async_computation.4 | async-start | bytes 8847360 | tf_op jit(solution)/shard_map/all_gather | solution.py:62
  511.7 183.8 %all-to-all-start = ((bf16[1536,2,2560]{0,2,1:T(8,128)(2,1)}), bf16[1536,2,2560]{0,2,1:T(8,128)(2,1)}, u32[]{:S(2)}, u32[]{:S(2)}) async-start(bf16[1536,2,2560]{0,2,1:T(8,128)(2,1)} %bitcast.59), calls=%async_computation | async-start | bytes 31457280 | tf_op jit(solution)/shard_map/all_to_all | solution.py:78
  521.1 193.7 %all-gather.14.cloned.1.call-start = ((), (), s32[]{:S(2)}) async-start(), calls=%async_computation.5 | async-start | bytes 2949120 | tf_op jit(solution)/shard_map/all_gather | solution.py:77
  677.0 3.3 copy-start.4
  677.0 3.3 copy-start.5
  680.0 136.1 %all-reduce.2.cloned.1.call-start = ((), (), s32[]{:S(2)}) async-start(), calls=%async_computation.6 | async-start | bytes 655360 | tf_op jit(solution)/shard_map/psum | solution.py:89
  714.8 9.4 %copy-start.1 = (bf16[2,1,160,2560]{3,2,1,0:T(8,128)(2,1)S(1)}, bf16[2,1,160,2560]{3,2,1,0:T(8,128)(2,1)}, u32[]{:S(2)}) copy-start(bf16[2,1,160,2560]{3,2,1,0:T(8,128)(2,1)} %param.9) | copy-start | bytes 4915204
  714.8 9.4 %copy-start.2 = (bf16[2,1,160,2560]{3,2,1,0:T(8,128)(2,1)S(1)}, bf16[2,1,160,2560]{3,2,1,0:T(8,128)(2,1)}, u32[]{:S(2)}) copy-start(bf16[2,1,160,2560]{3,2,1,0:T(8,128)(2,1)} %param.17) | copy-start | bytes 4915204
  714.8 9.4 %copy-start.3 = (bf16[2560]{0:T(1024)(128)(2,1)S(1)}, bf16[2560]{0:T(1024)(128)(2,1)}, u32[]{:S(2)}) copy-start(bf16[2560]{0:T(1024)(128)(2,1)} %param.11) | copy-start | bytes 15364
Sparse Core Ops, SparseCore 0:
  10.9 48.2 all-gather.5
  60.8 402.1 all-gather.7
  490.5 75.9 all-gather.9
  568.5 76.2 all-gather.11
  680.1 33.5 all-gather.13
  727.7 88.3 all-reduce.1
where the time goes:
time: 827 us; the launch traced here: 825 us
  waiting for transfers between devices  639 us (77%)
  local copies, waits for them, and re-layouts  91.2 us (11%)
  matrix products  62.8 us (8%)
  between operations  14.3 us (2%)
  starting transfers between devices  9.99 us (1%)
    all_gather x1, waiting for transfers between devices, body(): piece = lax.all_gather(w_qkv, 'frame', axis=0, tiled=True)  404 us
    psum x1, waiting for transfers between devices, body(): grad_proj = lax.psum(grad_terms, ('frame', 'dp'))  88.5 us
    all_gather x1, waiting for transfers between devices, body(): piece_values = lax.all_gather(own_values, 'frame', axis=1, tiled=True)  47 us
    all_gather x1, waiting for transfers between devices, body(): piece_keys = lax.all_gather(own_keys, 'frame', axis=1, tiled=True)  44.6 us
    all_gather x1, waiting for transfers between devices, body(): features = lax.all_gather(row_block, 'mp', axis=1, tiled=True)  39.5 us
    unnamed x17, local copies, waits for them, and re-layouts  32.5 us
    dot_general x1, matrix products, body(): jnp.dot(features, piece.reshape(count, 3 * heads_width), preferred_elemen...  24.1 us
    all_to_all x1, local copies, waits for them, and re-layouts, body(): lax.all_to_all(w_out, 'mp', split_axis=1, concat_axis=0, tiled=True)  19.3 us
  transfers between devices with their start and end apart: 7, of which 6 were waited for; matrix products, arithmetic and copies ran while one was open for 14% of the time, Pallas kernels for 0%

commit v1 on v0

v1 whole, which is shorter than its diff:
```python
import functools
import math

import jax
import jax.numpy as jnp
from jax import lax
from jax.experimental import pallas as pl
from jax.experimental.pallas import tpu as pltpu
from jax.sharding import PartitionSpec as P

HS = 128


def attend_kernel(frames, q_ref, k_ref, v_ref, o_ref):
    scale = 1.0 / math.sqrt(HS)
    for t in range(frames):
        q = q_ref[t].astype(jnp.float32) * scale
        scores = [
            jnp.sum(q * k_ref[u].astype(jnp.float32), axis=-1, keepdims=True) for u in range(t + 1)
        ]
        peak = functools.reduce(jnp.maximum, scores)
        weights = [jnp.exp(s - peak) for s in scores]
        total = functools.reduce(jnp.add, weights)
        accum = functools.reduce(
            jnp.add, [w * v_ref[u].astype(jnp.float32) for u, w in enumerate(weights)]
        )
        o_ref[t] = (accum / total).astype(o_ref.dtype)


def attend(qkv, frames, heads_width):
    rows = qkv.shape[1]
    heads = heads_width // HS
    spec = lambda part: pl.BlockSpec((frames, rows, HS), lambda h, part=part: (0, 0, part * heads + h))
    return pl.pallas_call(
        functools.partial(attend_kernel, frames),
        grid=(heads,),
        in_specs=[spec(0), spec(1), spec(2)],
        out_specs=spec(0),
        out_shape=jax.ShapeDtypeStruct((frames, rows, heads_width), jnp.bfloat16),
        cost_estimate=pl.CostEstimate(flops=4 * frames * frames * rows * heads_width,
                                      bytes_accessed=8 * frames * rows * heads_width,
                                      transcendentals=0),
        name="attend",
    )(qkv, qkv, qkv)


def gather_mp(block, size):
    if size != 2:
        return lax.all_gather(block, "mp", axis=block.ndim - 1, tiled=True)
    other = lax.ppermute(block, "mp", [(0, 1), (1, 0)])
    first = lax.axis_index("mp") == 0
    return jnp.concatenate(
        [jnp.where(first, block, other), jnp.where(first, other, block)], axis=-1
    )


def body(mp_size, dp_size, tokens, token_mask, mask_embed, w_qkv, w_out, action_idx, codebook,
         act_proj, cotangent):
    clips, _, spots, width = tokens.shape
    heads_width = w_qkv.shape[2]
    depth = w_qkv.shape[0]
    xin = jnp.where(token_mask[..., None] == 1, mask_embed, tokens)
    share = depth // dp_size
    mine = lax.dynamic_slice_in_dim(
        w_qkv.reshape(depth, 3 * heads_width), lax.axis_index("dp") * share, share, axis=0
    )
    weights = lax.all_gather(mine, ("frame", "dp"), axis=0, tiled=True)
    spread = lax.all_to_all(
        xin.reshape(clips, spots, width), "frame", split_axis=1, concat_axis=0, tiled=True
    )
    frames = spread.shape[0] // clips
    local = spread.shape[1]
    features = gather_mp(spread.reshape(frames * clips * local, width), mp_size)
    qkv = jnp.dot(features, weights, preferred_element_type=jnp.float32).astype(jnp.bfloat16)
    attn = attend(qkv.reshape(frames, clips * local, 3 * heads_width), frames, heads_width)
    back = lax.all_to_all(
        attn.reshape(frames * clips, local, heads_width), "frame", split_axis=0, concat_axis=1,
        tiled=True,
    )
    all_heads = gather_mp(back.reshape(clips * spots, heads_width), mp_size)
    out_block = lax.all_to_all(w_out, "mp", split_axis=1, concat_axis=0, tiled=True)
    mixed_rows = jnp.dot(all_heads, out_block, preferred_element_type=jnp.float32)
    mixed = mixed_rows.reshape(clips, 1, spots, width)
    onehot = (
        action_idx.reshape(clips)[:, None] == jnp.arange(codebook.shape[0])[None, :]
    ).astype(jnp.float32)
    codevec = jnp.dot(onehot, codebook, precision=lax.Precision.HIGHEST)
    gate = jnp.dot(codevec, act_proj, precision=lax.Precision.HIGHEST)
    next_state = (xin.astype(jnp.float32) + gate[:, None, None, :] * mixed).astype(jnp.bfloat16)
    dgate = jnp.sum(cotangent.astype(jnp.float32) * mixed, axis=2).reshape(clips, width)
    codes_all = lax.all_gather(codevec, ("frame", "dp"), axis=0, tiled=True)
    dgate_all = lax.all_gather(dgate, ("frame", "dp"), axis=0, tiled=True)
    grad_proj = jnp.dot(codes_all.T, dgate_all, precision=lax.Precision.HIGHEST)
    return (next_state, grad_proj)


def solution(mesh):
    in_specs = (
        P("dp", "frame", None, "mp"),
        P("dp", "frame", None),
        P("mp"),
        P("frame", None, "mp"),
        P("mp", None),
        P("dp", "frame"),
        P(),
        P(None, "mp"),
        P("dp", "frame", None, "mp"),
    )
    out_specs = (P("dp", "frame", None, "mp"), P(None, "mp"))
    return jax.shard_map(
        functools.partial(body, mesh.shape["mp"], mesh.shape["dp"]),
        mesh=mesh, in_specs=in_specs, out_specs=out_specs, check_vma=False,
    )
```

time: 827 us -> 643 us (0.78)
  waiting for transfers between devices: 639 us -> 345 us
  blocking collectives: 0 us -> 114 us
  matrix products: 62.8 us -> 34.1 us
  starting transfers between devices: 9.99 us -> 37.9 us
  local copies, waits for them, and re-layouts: 91.2 us -> 68.5 us
  Pallas kernels: 0 us -> 9.53 us
    all_gather x5 -> x1, waiting for transfers between devices: 535 us -> 162 us  [body(): weights = lax.all_gather(mine, ('frame', 'dp'), axis=0, tiled=True)]
    all_to_all x1, waiting for transfers between devices: 14.7 us -> 138 us  [body(): lax.all_to_all(w_out, 'mp', split_axis=1, concat_axis=0, tiled=True)]
    psum x1 -> x0, waiting for transfers between devices: 88.5 us -> none  [body(): grad_proj = lax.psum(grad_terms, ('frame', 'dp'))]
    all_gather x0 -> x2, blocking collectives: none -> 60.5 us  [the longest x1 31 us: body(): dgate_all = lax.all_gather(dgate, ('frame', 'dp'), axis=0, tiled=True)]
    all_to_all x0 -> x1, blocking collectives: none -> 53.6 us  [body(): lax.all_to_all(xin.reshape(clips, spots, width), 'frame', split_axis=1, c...]
    ppermute x0 -> x2, waiting for transfers between devices: none -> 37.1 us  [gather_mp(): other = lax.ppermute(block, 'mp', [(0, 1), (1, 0)])]
    dot_general x4 -> x2, matrix products: 53 us -> 24.9 us  [the longest x1 23.7 us: body(): jnp.dot(features, weights, preferred_element_type=jnp.float32)]
    reshape x3, local copies, waits for them, and re-layouts: 30.9 us -> 3.74 us  [the longest x1 2.14 us: body(): attn.reshape(frames * clips, local, heads_width)]
  transfers between devices with their start and end apart: 7 -> 5, of which waited for: 6 -> 5; matrix products, arithmetic and copies ran while one was open for 14% -> 8% of each run, Pallas kernels for 0% -> 0%
where the time goes in v1:
time: 643 us; the launch traced here: 638 us
  waiting for transfers between devices  345 us (54%)
  blocking collectives  114 us (18%)
  local copies, waits for them, and re-layouts  68.5 us (11%)
  starting transfers between devices  37.9 us (6%)
  matrix products  34.1 us (5%)
  other arithmetic  14.6 us (2%)
  between operations  14.2 us (2%)
  Pallas kernels  9.53 us (1%)
    all_gather x1, waiting for transfers between devices, body(): weights = lax.all_gather(mine, ('frame', 'dp'), axis=0, tiled=True)  162 us
    all_to_all x1, waiting for transfers between devices, body(): lax.all_to_all(w_out, 'mp', split_axis=1, concat_axis=0, tiled=True)  138 us
    all_to_all x1, blocking collectives, body(): lax.all_to_all(xin.reshape(clips, spots, width), 'frame', split_axis=1, c...  53.6 us
    ppermute x2, waiting for transfers between devices, gather_mp(): other = lax.ppermute(block, 'mp', [(0, 1), (1, 0)])  37.1 us
    unnamed x20, local copies, waits for them, and re-layouts  33.1 us
    all_gather x1, blocking collectives, body(): dgate_all = lax.all_gather(dgate, ('frame', 'dp'), axis=0, tiled=True)  31 us
    all_gather x1, blocking collectives, body(): codes_all = lax.all_gather(codevec, ('frame', 'dp'), axis=0, tiled=True)  29.5 us
    all_to_all x1, starting transfers between devices, body(): lax.all_to_all(attn.reshape(frames * clips, local, heads_width), 'frame',...  25.9 us
  transfers between devices with their start and end apart: 5, of which 5 were waited for; matrix products, arithmetic and copies ran while one was open for 8% of the time, Pallas kernels for 0%

profile of v1, /device:TPU:1, one launch (start us, length us, event | category | flops | bytes accessed | tf_op | source)
XLA Modules:
  0.0 638.2 jit_solution(1397826993860630567)
XLA Ops:
  7.2 0.0 copy-start
  7.2 0.0 all-gather.4.cloned.1.call-start
  7.2 9.0 %copy.30 = bf16[640,3,1536]{0,2,1:T(8,128)(2,1)} copy(bf16[640,3,1536]{2,0,1:T(8,128)(2,1)} %param.12) | data formatting | bytes 11796480 | tf_op args[3]
  16.2 6.2 constant_dynamic-slice_fusion
  22.4 5.6 copy.31
  28.0 0.0 copy-start.5
  28.0 0.0 copy-start.1
  28.0 0.0 copy-start.4
  28.0 0.0 all-gather.4.cloned.1.call-update
  28.0 0.7 copy-done.5
  28.6 0.1 copy.38
  28.8 0.6 copy-done.1
  29.4 0.0 copy-done.4
  29.4 2.0 fusion.9
  31.4 53.6 %all_to_all.49 = bf16[2,160,2560]{2,0,1:T(2,128)(2,1)S(1)} all-to-all(bf16[2,160,2560]{2,0,1:T(2,128)(2,1)S(1)} %fusion.9), channel_id=1, replica_groups=mesh['frame'=8,'mp'=2,'dp'=2] {'frame'}, dimensions={1} | all-to-all | bytes 3276800 | tf_op jit(solution)/shard_map/all_to_all | solution.py:68
  85.1 0.2 copy.29
  85.3 1.3 reshape.60
  86.6 1.2 collective-permute-start
  87.9 35.6 %collective-permute-done = bf16[320,2560]{1,0:T(8,128)(2,1)S(1)} collective-permute-done((bf16[320,2560]{1,0:T(8,128)(2,1)}, bf16[320,2560]{1,0:T(8,128)(2,1)S(1)}, u32[]{:S(2)}, u32[]{:S(2)}) %collective-permute-start) | collective-permute-done | bytes 1638432 | tf_op jit(solution)/shard_map/ppermute | solution.py:50
  123.5 3.4 broadcast_select_fusion.2
  126.8 162.1 %all-gather.4.cloned.1.call-done = bf16[5120,4608]{1,0:T(8,128)(2,1)} async-done(((bf16[320,4608]{1,0:T(8,128)(2,1)}), bf16[5120,4608]{1,0:T(8,128)(2,1)}) %all-gather.4.cloned.1.call-update) | async-done | bytes 47185936 | tf_op jit(solution)/shard_map/all_gather | solution.py:67
  288.9 23.7 %convolution_convert_fusion = bf16[320,4608]{1,0:T(8,128)(2,1)} fusion(bf16[5120,4608]{1,0:T(8,128)(2,1)} %all-gather.4.cloned.1.call-done, bf16[320,2560]{1,0:T(8,128)(2,1)} %get-tuple-element.5, bf16[320,2560]{1,0:T(8,128)(2,1)} %get-tuple-element.4), kind=kOutput, calls=%fused_computation | convolution fusion | flops 15107522560 | bytes 53411840 | tf_op jit(solution)/shard_map/dot_general | solution.py:74
  312.6 9.5 %attend.1 = bf16[8,40,1536]{2,1,0:T(8,128)(2,1)} custom-call(bf16[8,40,4608]{2,1,0:T(8,128)(2,1)} %bitcast.30, bf16[8,40,4608]{2,1,0:T(8,128)(2,1)} %bitcast.31, bf16[8,40,4608]{2,1,0:T(8,128)(2,1)} %bitcast.32), custom_call_target="tpu_custom_call" | custom-call | flops 15728640 | bytes 3932160 | tf_op jit(solution)/shard_map/attend/pallas_call | solution.py:34
  322.1 2.1 reshape.63
  324.3 25.9 %all-to-all-start.1 = ((bf16[16,20,1536]{2,1,0:T(8,128)(2,1)}), bf16[16,20,1536]{2,1,0:T(8,128)(2,1)S(1)}, u32[]{:S(2)}, u32[]{:S(2)}) async-start(bf16[16,20,1536]{2,1,0:T(8,128)(2,1)} %reshape.63), calls=%async_computation.1 | async-start | bytes 2359296 | tf_op jit(solution)/shard_map/all_to_all | solution.py:76
  350.1 20.6 %copy.33 = bf16[1536,5120]{0,1:T(8,128)(2,1)} copy(bf16[1536,5120]{1,0:T(8,128)(2,1)} %param.13) | data formatting | bytes 31457280 | tf_op args[4]
  370.7 7.8 %all-to-all-done.1 = bf16[16,20,1536]{2,1,0:T(8,128)(2,1)S(1)} async-done(((bf16[16,20,1536]{2,1,0:T(8,128)(2,1)}), bf16[16,20,1536]{2,1,0:T(8,128)(2,1)S(1)}, u32[]{:S(2)}, u32[]{:S(2)}) %all-to-all-start.1) | async-done | bytes 983072 | tf_op jit(solution)/shard_map/all_to_all | solution.py:76
  378.5 9.3 %all-to-all-start.2 = ((bf16[1536,2,2560]{0,2,1:T(8,128)(2,1)}), bf16[1536,2,2560]{0,2,1:T(8,128)(2,1)}, u32[]{:S(2)}, u32[]{:S(2)}) async-start(bf16[1536,2,2560]{0,2,1:T(8,128)(2,1)} %bitcast.29), calls=%async_computation.2 | async-start | bytes 31457280 | tf_op jit(solution)/shard_map/all_to_all | solution.py:81
  387.9 0.0 copy-start.6
  387.9 0.0 copy-start.7
  387.9 0.1 copy.50
  388.0 0.3 reshape.64
  388.2 1.5 collective-permute-start.1
  389.7 0.0 copy-done.6
  389.7 0.0 copy-done.7
  389.7 0.2 fusion.10
  389.9 29.5 %all-gather = f32[16,2,32]{2,1,0:T(2,128)S(1)} all-gather(f32[1,2,32]{2,1,0:T(2,128)S(1)} %bitcast.44), channel_id=1, replica_groups=mesh['frame'=8,'mp'=2,'dp'=2] {'frame','dp'}, dimensions={0}, use_global_device_ids=true | all-gather | bytes 4352 | tf_op jit(solution)/shard_map/all_gather | solution.py:91
  419.4 0.0 copy-done
  419.4 0.3 fusion.16
  419.7 138.3 %all-to-all-done.2 = bf16[1536,2,2560]{0,2,1:T(8,128)(2,1)} async-done(((bf16[1536,2,2560]{0,2,1:T(8,128)(2,1)}), bf16[1536,2,2560]{0,2,1:T(8,128)(2,1)}, u32[]{:S(2)}, u32[]{:S(2)}) %all-to-all-start.2) | async-done | bytes 15728672 | tf_op jit(solution)/shard_map/all_to_all | solution.py:81
  558.0 19.5 %copy.34 = bf16[2,1536,2560]{2,1,0:T(8,128)(2,1)} copy(bf16[2,1536,2560]{1,2,0:T(8,128)(2,1)} %bitcast.10) | data formatting | bytes 31457280 | tf_op jit(solution)/shard_map/all_to_all | solution.py:81
  577.5 1.5 collective-permute-done.1
  578.9 0.1 broadcast_select_fusion.4
  579.1 0.0 copy-start.2
  579.1 8.8 %fusion.5 = f32[320,2560]{1,0:T(8,128)S(1)} fusion(bf16[3072,2560]{1,0:T(8,128)(2,1)} %bitcast.33, bf16[320,1536]{1,0:T(8,128)(2,1)S(1)} %get-tuple-element.7, bf16[320,1536]{1,0:T(8,128)(2,1)S(1)} %get-tuple-element.6), kind=kOutput, calls=%fused_computation.9 | convolution fusion | flops 5037096960 | bytes 20971520 | tf_op jit(solution)/shard_map/dot_general | solution.py:82
  587.9 0.0 copy-done.2
  587.9 8.6 %fusion.4 = bf16[2,1,160,2560]{3,0,2,1:T(2,128)(2,1)S(1)} fusion(f32[2,1,160,2560]{3,2,0,1:T(8,128)S(1)} %bitcast.35, f32[2,2560]{1,0:T(2,128)S(1)} %fusion.16, bf16[2,1,160,2560]{3,2,1,0:T(8,128)(2,1)S(1)} %copy-done.2, bf16[2560]{0:T(1024)(128)(2,1)S(1)} %copy-done.4, pred[2,160]{0,1:T(8,128)(4,1)S(1)} %bitcast.41), kind=kLoop, calls=%fused_computation.6 | loop fusion | flops 4096000 | bytes 6579520 | tf_op jit(solution)/shard_map/convert_element_type | solution.py:89
  596.5 0.0 copy-start.3
  596.5 1.3 copy.37
  597.8 0.7 copy-done.3
  598.5 0.4 multiply_reduce_fusion
  598.9 31.0 %all-gather.1 = f32[16,2,2560]{2,1,0:T(2,128)S(1)} all-gather(f32[1,2,2560]{2,1,0:T(2,128)S(1)} %bitcast.42), channel_id=1, replica_groups=mesh['frame'=8,'mp'=2,'dp'=2] {'frame','dp'}, dimensions={0}, use_global_device_ids=true | all-gather | bytes 348160 | tf_op jit(solution)/shard_map/all_gather | solution.py:92
  630.0 0.2 reshape.69
  630.2 1.2 fusion.17
  (1 shorter events, 0.0 us)
Async XLA Ops:
  7.2 412.2 %copy-start = (f32[32,2560]{1,0:T(8,128)S(1)}, f32[32,2560]{1,0:T(8,128)}, u32[]{:S(2)}) copy-start(f32[32,2560]{1,0:T(8,128)} %param.16) | copy-start | bytes 983044
  7.2 281.7 %all-gather.4.cloned.1.call-start = ((), (), s32[]{:S(2)}) async-start(), calls=%async_computation.3 | async-start | bytes 50135040 | tf_op jit(solution)/shard_map/all_gather | solution.py:67
  28.0 0.7 copy-start.5
  28.0 1.4 copy-start.1
  28.0 1.4 copy-start.4
  86.6 36.8 %collective-permute-start = (bf16[320,2560]{1,0:T(8,128)(2,1)}, bf16[320,2560]{1,0:T(8,128)(2,1)S(1)}, u32[]{:S(2)}, u32[]{:S(2)}) collective-permute-start(bf16[320,2560]{1,0:T(8,128)(2,1)} %reshape.60), channel_id=1, source_target_pairs={{0,2},{2,0},{1,3},{3,1},{4,6},{6,4},{5,7},{7,5},{8,10},{10,8},{9,1... | collective-permute-start | bytes 4915208 | tf_op jit(solution)/shard_map/ppermute | solution.py:50
  324.3 54.3 %all-to-all-start.1 = ((bf16[16,20,1536]{2,1,0:T(8,128)(2,1)}), bf16[16,20,1536]{2,1,0:T(8,128)(2,1)S(1)}, u32[]{:S(2)}, u32[]{:S(2)}) async-start(bf16[16,20,1536]{2,1,0:T(8,128)(2,1)} %reshape.63), calls=%async_computation.1 | async-start | bytes 2359296 | tf_op jit(solution)/shard_map/all_to_all | solution.py:76
  378.5 179.4 %all-to-all-start.2 = ((bf16[1536,2,2560]{0,2,1:T(8,128)(2,1)}), bf16[1536,2,2560]{0,2,1:T(8,128)(2,1)}, u32[]{:S(2)}, u32[]{:S(2)}) async-start(bf16[1536,2,2560]{0,2,1:T(8,128)(2,1)} %bitcast.29), calls=%async_computation.2 | async-start | bytes 31457280 | tf_op jit(solution)/shard_map/all_to_all | solution.py:81
  387.9 1.9 copy-start.6
  387.9 1.9 copy-start.7
  388.2 190.7 %collective-permute-start.1 = (bf16[320,1536]{1,0:T(8,128)(2,1)S(1)}, bf16[320,1536]{1,0:T(8,128)(2,1)S(1)}, u32[]{:S(2)}, u32[]{:S(2)}) collective-permute-start(bf16[320,1536]{1,0:T(8,128)(2,1)S(1)} %reshape.64), channel_id=1, source_target_pairs={{0,2},{2,0},{1,3},{3,1},{4,6},{6,4},{5,7},{7,5},{8,10},{10,8},{9,1... | collective-permute-start | bytes 2949128 | tf_op jit(solution)/shard_map/ppermute | solution.py:50
  579.1 8.8 %copy-start.2 = (bf16[2,1,160,2560]{3,2,1,0:T(8,128)(2,1)S(1)}, bf16[2,1,160,2560]{3,2,1,0:T(8,128)(2,1)}, u32[]{:S(2)}) copy-start(bf16[2,1,160,2560]{3,2,1,0:T(8,128)(2,1)} %param.9) | copy-start | bytes 4915204
  596.5 2.0 copy-start.3
Sparse Core Ops, SparseCore 0:
  28.1 260.7 all-gather.3

commit v2 on v1

--- a/solution.py
+++ b/solution.py
@@ -44,6 +44,48 @@
     )(qkv, qkv, qkv)
 
 
+def spread_kernel(frames, dps, x_ref, o_ref, send_sem, recv_sem, own_sem):
+    count = frames * dps
+    me = lax.axis_index("frame") * dps + lax.axis_index("dp")
+    barrier = pltpu.get_barrier_semaphore()
+
+    def peer(shift):
+        other = lax.rem(me + shift, count)
+        return {"frame": other // dps, "dp": lax.rem(other, dps)}
+
+    for shift in range(1, count):
+        pl.semaphore_signal(barrier, inc=1, device_id=peer(shift),
+                            device_id_type=pl.DeviceIdType.MESH)
+    own = pltpu.make_async_copy(x_ref, o_ref.at[me], own_sem)
+    own.start()
+    pl.semaphore_wait(barrier, count - 1)
+    copies = []
+    for shift in range(1, count):
+        copy = pltpu.make_async_remote_copy(
+            src_ref=x_ref, dst_ref=o_ref.at[me], send_sem=send_sem.at[shift],
+            recv_sem=recv_sem.at[shift], device_id=peer(shift),
+            device_id_type=pl.DeviceIdType.MESH)
+        copy.start()
+        copies.append(copy)
+    own.wait()
+    for copy in copies:
+        copy.wait()
+
+
+def spread_terms(terms, frames, dps):
+    count = frames * dps
+    return pl.pallas_call(
+        functools.partial(spread_kernel, frames, dps),
+        in_specs=[pl.BlockSpec(memory_space=pltpu.VMEM)],
+        out_specs=pl.BlockSpec(memory_space=pltpu.VMEM),
+        out_shape=jax.ShapeDtypeStruct((count, *terms.shape), terms.dtype),
+        scratch_shapes=[pltpu.SemaphoreType.DMA((count,)), pltpu.SemaphoreType.DMA((count,)),
+                        pltpu.SemaphoreType.DMA],
+        compiler_params=pltpu.CompilerParams(collective_id=1, has_side_effects=True),
+        name="spread_terms",
+    )(terms)
+
+
 def gather_mp(block, size):
     if size != 2:
         return lax.all_gather(block, "mp", axis=block.ndim - 1, tiled=True)
@@ -65,6 +107,12 @@
         w_qkv.reshape(depth, 3 * heads_width), lax.axis_index("dp") * share, share, axis=0
     )
     weights = lax.all_gather(mine, ("frame", "dp"), axis=0, tiled=True)
+    if mp_size == 2:
+        my_mp = lax.axis_index("mp")
+        out_mine = lax.dynamic_slice_in_dim(w_out, my_mp * width, width, axis=1)
+        out_other = lax.ppermute(
+            lax.dynamic_slice_in_dim(w_out, (1 - my_mp) * width, width, axis=1),
+            "mp", [(0, 1), (1, 0)])
     spread = lax.all_to_all(
         xin.reshape(clips, spots, width), "frame", split_axis=1, concat_axis=0, tiled=True
     )
@@ -77,9 +125,15 @@
         attn.reshape(frames * clips, local, heads_width), "frame", split_axis=0, concat_axis=1,
         tiled=True,
     )
-    all_heads = gather_mp(back.reshape(clips * spots, heads_width), mp_size)
-    out_block = lax.all_to_all(w_out, "mp", split_axis=1, concat_axis=0, tiled=True)
-    mixed_rows = jnp.dot(all_heads, out_block, preferred_element_type=jnp.float32)
+    heads = back.reshape(clips * spots, heads_width)
+    if mp_size == 2:
+        other_heads = lax.ppermute(heads, "mp", [(0, 1), (1, 0)])
+        mixed_rows = jnp.dot(heads, out_mine, preferred_element_type=jnp.float32) + jnp.dot(
+            other_heads, out_other, preferred_element_type=jnp.float32)
+    else:
+        out_block = lax.all_to_all(w_out, "mp", split_axis=1, concat_axis=0, tiled=True)
+        mixed_rows = jnp.dot(gather_mp(heads, mp_size), out_block,
+                             preferred_element_type=jnp.float32)
     mixed = mixed_rows.reshape(clips, 1, spots, width)
     onehot = (
         action_idx.reshape(clips)[:, None] == jnp.arange(codebook.shape[0])[None, :]
@@ -88,9 +142,12 @@
     gate = jnp.dot(codevec, act_proj, precision=lax.Precision.HIGHEST)
     next_state = (xin.astype(jnp.float32) + gate[:, None, None, :] * mixed).astype(jnp.bfloat16)
     dgate = jnp.sum(cotangent.astype(jnp.float32) * mixed, axis=2).reshape(clips, width)
-    codes_all = lax.all_gather(codevec, ("frame", "dp"), axis=0, tiled=True)
-    dgate_all = lax.all_gather(dgate, ("frame", "dp"), axis=0, tiled=True)
-    grad_proj = jnp.dot(codes_all.T, dgate_all, precision=lax.Precision.HIGHEST)
+    codes = codevec.shape[1]
+    padded = jnp.pad(codevec, ((0, 0), (0, -codes % 128)))
+    terms = spread_terms(jnp.concatenate([dgate, padded], axis=1), frames, dp_size)
+    terms = terms.reshape(frames * dp_size * clips, -1)
+    grad_proj = jnp.dot(
+        terms[:, width : width + codes].T, terms[:, :width], precision=lax.Precision.HIGHEST)
     return (next_state, grad_proj)
 
 

time: 643 us -> 442 us (0.69)
  blocking collectives: 114 us -> 0 us
  waiting for transfers between devices: 345 us -> 279 us
  local copies, waits for them, and re-layouts: 68.5 us -> 38 us
  Pallas kernels: 9.53 us -> 22.9 us
    all_to_all x1, waiting for transfers between devices: 138 us -> 47.4 us  [body(): lax.all_to_all(xin.reshape(clips, spots, width), 'frame', split_axis=1, c...]
    all_gather x2 -> x0, blocking collectives: 60.5 us -> none  [the longest x1 31 us: body(): dgate_all = lax.all_gather(dgate, ('frame', 'dp'), axis=0, tiled=True)]
    all_to_all x1 -> x0, blocking collectives: 53.6 us -> none  [body(): lax.all_to_all(xin.reshape(clips, spots, width), 'frame', split_axis=1, c...]
    unnamed x20 -> x22, local copies, waits for them, and re-layouts: 33.1 us -> 12.2 us
    all_to_all x1, waiting for transfers between devices: 7.83 us -> 28.4 us  [body(): lax.all_to_all(attn.reshape(frames * clips, local, heads_width), 'frame',...]
    all_to_all x1 -> x0, local copies, waits for them, and re-layouts: 19.5 us -> none  [body(): lax.all_to_all(w_out, 'mp', split_axis=1, concat_axis=0, tiled=True)]
    ppermute x0 -> x2, waiting for transfers between devices: none -> 15.6 us  [the longest x1 15.6 us: body(): other_heads = lax.ppermute(heads, 'mp', [(0, 1), (1, 0)])]
    pallas_call x0 -> x1, Pallas kernels: none -> 13.4 us  [spread_terms(): pl.pallas_call(functools.partial(spread_kernel, frames, dps), in_specs=[p...]
  transfers between devices with their start and end apart: 5 -> 6, of which waited for: 5 -> 5; matrix products, arithmetic and copies ran while one was open for 8% -> 11% of each run, Pallas kernels for 0% -> 2%
where the time goes in v2:
time: 442 us; the launch traced here: 441 us
  waiting for transfers between devices  279 us (63%)
  local copies, waits for them, and re-layouts  38 us (9%)
  matrix products  35.5 us (8%)
  starting transfers between devices  35.2 us (8%)
  Pallas kernels  22.9 us (5%)
  other arithmetic  16.4 us (4%)
  between operations  14.2 us (3%)
    all_gather x1, waiting for transfers between devices, body(): weights = lax.all_gather(mine, ('frame', 'dp'), axis=0, tiled=True)  159 us
    all_to_all x1, waiting for transfers between devices, body(): lax.all_to_all(xin.reshape(clips, spots, width), 'frame', split_axis=1, c...  47.4 us
    all_to_all x1, waiting for transfers between devices, body(): lax.all_to_all(attn.reshape(frames * clips, local, heads_width), 'frame',...  28.4 us
    ppermute x1, waiting for transfers between devices, gather_mp(): other = lax.ppermute(block, 'mp', [(0, 1), (1, 0)])  28.1 us
    all_to_all x1, starting transfers between devices, body(): lax.all_to_all(attn.reshape(frames * clips, local, heads_width), 'frame',...  26 us
    dot_general x1, matrix products, body(): jnp.dot(features, weights, preferred_element_type=jnp.float32)  23.8 us
    ppermute x1, waiting for transfers between devices, body(): other_heads = lax.ppermute(heads, 'mp', [(0, 1), (1, 0)])  15.6 us
    pallas_call x1, Pallas kernels, spread_terms(): pl.pallas_call(functools.partial(spread_kernel, frames, dps), in_specs=[p...  13.4 us
  transfers between devices with their start and end apart: 6, of which 5 were waited for; matrix products, arithmetic and copies ran while one was open for 11% of the time, Pallas kernels for 2%

profile of v2, /device:TPU:1, one launch (start us, length us, event | category | flops | bytes accessed | tf_op | source)
XLA Modules:
  0.0 441.1 jit_solution(3602925788211797718)
XLA Ops:
  7.2 0.0 copy-start
  7.2 0.0 all-gather.2.cloned.1.call-start
  7.2 9.0 %copy.22 = bf16[640,3,1536]{0,2,1:T(8,128)(2,1)} copy(bf16[640,3,1536]{2,0,1:T(8,128)(2,1)} %param.12) | data formatting | bytes 11796480 | tf_op args[3]
  16.2 6.2 %constant_dynamic-slice_fusion.1 = bf16[320,4608]{0,1:T(8,128)(2,1)} fusion(bf16[640,4608]{0,1:T(8,128)(2,1)} %bitcast.26, s32[]{:T(128)S(6)} %select_n.29), kind=kLoop, calls=%fused_computation.27 | loop fusion | bytes 5898244 | tf_op jit(solution)/shard_map/dynamic_slice | solution.py:106
  22.4 0.0 copy-start.7
  22.4 0.0 copy-start.2
  22.4 0.0 copy-start.6
  22.4 5.7 %copy.23 = bf16[320,4608]{1,0:T(8,128)(2,1)} copy(bf16[320,4608]{0,1:T(8,128)(2,1)} %constant_dynamic-slice_fusion.1) | data formatting | bytes 5898240 | tf_op jit(solution)/shard_map/dynamic_slice | solution.py:106
  28.1 0.0 all-gather.2.cloned.1.call-update
  28.1 0.0 copy-done.7
  28.1 0.1 copy.28
  28.3 0.0 copy-done.2
  28.3 0.0 copy-done.6
  28.3 3.2 fusion.9
  31.5 6.4 %all-to-all-start = ((bf16[2,160,2560]{2,0,1:T(2,128)(2,1)}), bf16[2,160,2560]{2,0,1:T(2,128)(2,1)S(1)}, u32[]{:S(2)}, u32[]{:S(2)}) async-start(bf16[2,160,2560]{2,0,1:T(2,128)(2,1)} %fusion.9), calls=%async_computation | async-start | bytes 3276800 | tf_op jit(solution)/shard_map/all_to_all | solution.py:116
  37.9 47.4 %all-to-all-done = bf16[2,160,2560]{2,0,1:T(2,128)(2,1)S(1)} async-done(((bf16[2,160,2560]{2,0,1:T(2,128)(2,1)}), bf16[2,160,2560]{2,0,1:T(2,128)(2,1)S(1)}, u32[]{:S(2)}, u32[]{:S(2)}) %all-to-all-start) | async-done | bytes 1638432 | tf_op jit(solution)/shard_map/all_to_all | solution.py:116
  85.3 0.0 copy-start.1
  85.3 1.2 copy-done.1
  86.4 1.7 copy.21
  88.1 1.3 reshape.60
  89.5 0.0 copy-start.4
  89.5 1.2 collective-permute-start
  90.7 7.1 %constant_dynamic-slice_fusion = bf16[1536,2560]{1,0:T(8,128)(2,1)} fusion(bf16[1536,5120]{1,0:T(8,128)(2,1)} %param.13, s32[]{:T(128)S(6)} %select_n.31), kind=kLoop, calls=%fused_computation.25 | loop fusion | bytes 15728644 | tf_op jit(solution)/shard_map/dynamic_slice | solution.py:114
  97.8 0.4 collective-permute-start.2
  98.1 28.1 %collective-permute-done = bf16[320,2560]{1,0:T(8,128)(2,1)} collective-permute-done((bf16[320,2560]{1,0:T(8,128)(2,1)}, bf16[320,2560]{1,0:T(8,128)(2,1)}, u32[]{:S(2)}, u32[]{:S(2)}) %collective-permute-start) | collective-permute-done | bytes 1638432 | tf_op jit(solution)/shard_map/ppermute | solution.py:92
  126.2 0.0 copy-done.4
  126.2 3.5 broadcast_select_fusion.2
  129.7 159.3 %all-gather.2.cloned.1.call-done = bf16[5120,4608]{1,0:T(8,128)(2,1)} async-done(((bf16[320,4608]{1,0:T(8,128)(2,1)}), bf16[5120,4608]{1,0:T(8,128)(2,1)}) %all-gather.2.cloned.1.call-update) | async-done | bytes 47185936 | tf_op jit(solution)/shard_map/all_gather | solution.py:109
  289.0 23.8 %convolution_convert_fusion = bf16[320,4608]{1,0:T(8,128)(2,1)} fusion(bf16[5120,4608]{1,0:T(8,128)(2,1)} %all-gather.2.cloned.1.call-done, bf16[320,2560]{1,0:T(8,128)(2,1)} %get-tuple-element.5, bf16[320,2560]{1,0:T(8,128)(2,1)} %get-tuple-element.4), kind=kOutput, calls=%fused_computation.2 | convolution fusion | flops 15107522560 | bytes 53411840 | tf_op jit(solution)/shard_map/dot_general | solution.py:122
  312.8 9.5 %attend.1 = bf16[8,40,1536]{2,1,0:T(8,128)(2,1)} custom-call(bf16[8,40,4608]{2,1,0:T(8,128)(2,1)} %bitcast.23, bf16[8,40,4608]{2,1,0:T(8,128)(2,1)} %bitcast.24, bf16[8,40,4608]{2,1,0:T(8,128)(2,1)} %bitcast.25), custom_call_target="tpu_custom_call" | custom-call | flops 15728640 | bytes 3932160 | tf_op jit(solution)/shard_map/attend/pallas_call | solution.py:34
  322.3 2.1 reshape.63
  324.5 0.0 copy-start.8
  324.5 0.0 copy-start.9
  324.5 26.0 %all-to-all-start.1 = ((bf16[16,20,1536]{2,1,0:T(8,128)(2,1)}), bf16[16,20,1536]{2,1,0:T(8,128)(2,1)S(1)}, u32[]{:S(2)}, u32[]{:S(2)}) async-start(bf16[16,20,1536]{2,1,0:T(8,128)(2,1)} %reshape.63), calls=%async_computation.1 | async-start | bytes 2359296 | tf_op jit(solution)/shard_map/all_to_all | solution.py:124
  350.5 28.4 %all-to-all-done.1 = bf16[16,20,1536]{2,1,0:T(8,128)(2,1)S(1)} async-done(((bf16[16,20,1536]{2,1,0:T(8,128)(2,1)}), bf16[16,20,1536]{2,1,0:T(8,128)(2,1)S(1)}, u32[]{:S(2)}, u32[]{:S(2)}) %all-to-all-start.1) | async-done | bytes 983072 | tf_op jit(solution)/shard_map/all_to_all | solution.py:124
  378.9 0.1 copy.40
  379.0 0.3 reshape.64
  379.2 1.3 collective-permute-start.1
  380.5 0.0 copy-done.8
  380.5 0.0 copy-done.9
  380.5 0.2 fusion.12
  380.7 0.0 copy-done
  380.7 0.3 fusion.18
  381.0 5.0 %fusion = f32[320,2560]{1,0:T(8,128)S(1)} fusion(bf16[320,1536]{1,0:T(8,128)(2,1)S(1)} %reshape.64, bf16[1536,5120]{1,0:T(8,128)(2,1)} %param.13, s32[]{:T(128)S(6)} %select_n.30), kind=kOutput, calls=%fused_computation | convolution fusion | flops 2516582400 | bytes 12124164 | tf_op jit(solution)/shard_map/dot_general | solution.py:131
  386.0 0.0 copy-start.3
  386.0 0.0 collective-permute-done.2
  386.0 15.6 %collective-permute-done.1 = bf16[320,1536]{1,0:T(8,128)(2,1)S(1)} collective-permute-done((bf16[320,1536]{1,0:T(8,128)(2,1)S(1)}, bf16[320,1536]{1,0:T(8,128)(2,1)S(1)}, u32[]{:S(2)}, u32[]{:S(2)}) %collective-permute-start.1) | collective-permute-done | bytes 983072 | tf_op jit(solution)/shard_map/ppermute | solution.py:130
  401.6 5.0 %convolution_add_fusion = f32[320,2560]{1,0:T(8,128)S(1)} fusion(f32[320,2560]{1,0:T(8,128)S(1)} %fusion, bf16[320,1536]{1,0:T(8,128)(2,1)S(1)} %collective-permute-done.1, bf16[1536,2560]{1,0:T(8,128)(2,1)} %collective-permute-done.2), kind=kOutput, calls=%fused_computation.3 | convolution fusion | flops 2517401600 | bytes 15400960 | tf_op jit(solution)/shard_map/dot_general | solution.py:131
  406.7 0.0 copy-done.3
  406.7 8.6 %fusion.6 = bf16[2,1,160,2560]{3,0,2,1:T(2,128)(2,1)S(1)} fusion(f32[2,1,160,2560]{3,2,0,1:T(8,128)S(1)} %bitcast.27, f32[2,2560]{1,0:T(2,128)S(1)} %fusion.18, bf16[2,1,160,2560]{3,2,1,0:T(8,128)(2,1)S(1)} %copy-done.3, bf16[2560]{0:T(1024)(128)(2,1)S(1)} %copy-done.6, pred[2,160]{0,1:T(8,128)(4,1)S(1)} %bitcast.33), kind=kLoop, calls=%fused_computation.9 | loop fusion | flops 4096000 | bytes 6579520 | tf_op jit(solution)/shard_map/convert_element_type | solution.py:143
  415.3 0.0 copy-start.5
  415.3 1.3 copy.27
  416.6 0.7 copy-done.5
  417.3 0.5 multiply_reduce_fusion
  417.8 0.6 fusion.10.x_ref
  418.4 13.4 %spread_terms.1 = f32[16,2,2688]{2,1,0:T(2,128)} custom-call(f32[2,2688]{1,0:T(2,128)} %fusion.10.x_ref), custom_call_target="tpu_custom_call" | custom-call | tf_op jit(solution)/shard_map/spread_terms/pallas_call | solution.py:77
  431.8 1.2 reshape.66
  433.0 1.2 fusion.7
  (1 shorter events, 0.0 us)
Async XLA Ops:
  7.2 373.5 %copy-start = (f32[32,2560]{1,0:T(8,128)S(1)}, f32[32,2560]{1,0:T(8,128)}, u32[]{:S(2)}) copy-start(f32[32,2560]{1,0:T(8,128)} %param.16) | copy-start | bytes 983044
  7.2 281.8 %all-gather.2.cloned.1.call-start = ((), (), s32[]{:S(2)}) async-start(), calls=%async_computation.2 | async-start | bytes 50135040 | tf_op jit(solution)/shard_map/all_gather | solution.py:109
  22.4 5.7 %copy-start.7 = (s32[2,1,160]{2,1,0:T(1,128)S(1)}, s32[2,1,160]{2,1,0:T(1,128)}, u32[]{:S(2)}) copy-start(s32[2,1,160]{2,1,0:T(1,128)} %param.10) | copy-start | bytes 3844
  22.4 5.9 %copy-start.2 = (bf16[2,1,160,2560]{3,2,1,0:T(8,128)(2,1)S(1)}, bf16[2,1,160,2560]{3,2,1,0:T(8,128)(2,1)}, u32[]{:S(2)}) copy-start(bf16[2,1,160,2560]{3,2,1,0:T(8,128)(2,1)} %param.9) | copy-start | bytes 4915204
  22.4 5.9 %copy-start.6 = (bf16[2560]{0:T(1024)(128)(2,1)S(1)}, bf16[2560]{0:T(1024)(128)(2,1)}, u32[]{:S(2)}) copy-start(bf16[2560]{0:T(1024)(128)(2,1)} %param.11) | copy-start | bytes 15364
  31.5 53.8 %all-to-all-start = ((bf16[2,160,2560]{2,0,1:T(2,128)(2,1)}), bf16[2,160,2560]{2,0,1:T(2,128)(2,1)S(1)}, u32[]{:S(2)}, u32[]{:S(2)}) async-start(bf16[2,160,2560]{2,0,1:T(2,128)(2,1)} %fusion.9), calls=%async_computation | async-start | bytes 3276800 | tf_op jit(solution)/shard_map/all_to_all | solution.py:116
  85.3 1.2 copy-start.1
  89.5 36.8 %copy-start.4 = (bf16[320,2560]{1,0:T(8,128)(2,1)S(1)}, bf16[320,2560]{1,0:T(8,128)(2,1)}, u32[]{:S(2)}) copy-start(bf16[320,2560]{1,0:T(8,128)(2,1)} %reshape.60) | copy-start | bytes 4915204
  89.5 36.8 %collective-permute-start = (bf16[320,2560]{1,0:T(8,128)(2,1)}, bf16[320,2560]{1,0:T(8,128)(2,1)}, u32[]{:S(2)}, u32[]{:S(2)}) collective-permute-start(bf16[320,2560]{1,0:T(8,128)(2,1)} %reshape.60), channel_id=1, source_target_pairs={{0,2},{2,0},{1,3},{3,1},{4,6},{6,4},{5,7},{7,5},{8,10},{10,8},{9,1... | collective-permute-start | bytes 4915208 | tf_op jit(solution)/shard_map/ppermute | solution.py:92
  97.8 288.2 %collective-permute-start.2 = (bf16[1536,2560]{1,0:T(8,128)(2,1)}, bf16[1536,2560]{1,0:T(8,128)(2,1)}, u32[]{:S(2)}, u32[]{:S(2)}) collective-permute-start(bf16[1536,2560]{1,0:T(8,128)(2,1)} %constant_dynamic-slice_fusion), channel_id=1, source_target_pairs={{0,2},{2,0},{1,3},{3,1},{4,6},{6,4},{5,7},{7,5},{8,10},{10,8},{9,1... | collective-permute-start | bytes 23592968 | tf_op jit(solution)/shard_map/ppermute | solution.py:113
  324.5 56.0 %copy-start.8 = (f32[8,32]{1,0:T(8,128)S(1)}, f32[8,32]{1,0:T(8,128)}, u32[]{:S(2)}) copy-start(f32[8,32]{1,0:T(8,128)} %param.15) | copy-start | bytes 3076
  324.5 56.0 %copy-start.9 = (s32[2,1]{0,1:T(1,128)S(1)}, s32[2,1]{0,1:T(1,128)}, u32[]{:S(2)}) copy-start(s32[2,1]{0,1:T(1,128)} %param.14) | copy-start | bytes 28
  324.5 54.4 %all-to-all-start.1 = ((bf16[16,20,1536]{2,1,0:T(8,128)(2,1)}), bf16[16,20,1536]{2,1,0:T(8,128)(2,1)S(1)}, u32[]{:S(2)}, u32[]{:S(2)}) async-start(bf16[16,20,1536]{2,1,0:T(8,128)(2,1)} %reshape.63), calls=%async_computation.1 | async-start | bytes 2359296 | tf_op jit(solution)/shard_map/all_to_all | solution.py:124
  379.2 22.4 %collective-permute-start.1 = (bf16[320,1536]{1,0:T(8,128)(2,1)S(1)}, bf16[320,1536]{1,0:T(8,128)(2,1)S(1)}, u32[]{:S(2)}, u32[]{:S(2)}) collective-permute-start(bf16[320,1536]{1,0:T(8,128)(2,1)S(1)} %reshape.64), channel_id=1, source_target_pairs={{0,2},{2,0},{1,3},{3,1},{4,6},{6,4},{5,7},{7,5},{8,10},{10,8},{9,1... | collective-permute-start | bytes 2949128 | tf_op jit(solution)/shard_map/ppermute | solution.py:130
  386.0 20.7 %copy-start.3 = (bf16[2,1,160,2560]{3,2,1,0:T(8,128)(2,1)S(1)}, bf16[2,1,160,2560]{3,2,1,0:T(8,128)(2,1)}, u32[]{:S(2)}) copy-start(bf16[2,1,160,2560]{3,2,1,0:T(8,128)(2,1)} %param.9) | copy-start | bytes 4915204
  415.3 2.0 copy-start.5
Sparse Core Ops, SparseCore 0:
  28.2 260.7 all-gather.1

commit v3 on v2

--- a/solution.py
+++ b/solution.py
@@ -27,21 +27,21 @@
         o_ref[t] = (accum / total).astype(o_ref.dtype)
 
 
-def attend(qkv, frames, heads_width):
-    rows = qkv.shape[1]
+def attend(query, keys, values):
+    frames, rows, heads_width = query.shape
     heads = heads_width // HS
-    spec = lambda part: pl.BlockSpec((frames, rows, HS), lambda h, part=part: (0, 0, part * heads + h))
+    spec = pl.BlockSpec((frames, rows, HS), lambda h: (0, 0, h))
     return pl.pallas_call(
         functools.partial(attend_kernel, frames),
         grid=(heads,),
-        in_specs=[spec(0), spec(1), spec(2)],
-        out_specs=spec(0),
+        in_specs=[spec] * 3,
+        out_specs=spec,
         out_shape=jax.ShapeDtypeStruct((frames, rows, heads_width), jnp.bfloat16),
         cost_estimate=pl.CostEstimate(flops=4 * frames * frames * rows * heads_width,
                                       bytes_accessed=8 * frames * rows * heads_width,
                                       transcendentals=0),
         name="attend",
-    )(qkv, qkv, qkv)
+    )(query, keys, values)
 
 
 def spread_kernel(frames, dps, x_ref, o_ref, send_sem, recv_sem, own_sem):
@@ -86,6 +86,61 @@
     )(terms)
 
 
+def return_kernel(frames, x_ref, mine_ref, other_ref, send_sem, recv_sem, fwd_send, fwd_recv,
+                  own_sem):
+    me = lax.axis_index("frame")
+    across = {"mp": 1 - lax.axis_index("mp")}
+    barrier = pltpu.get_barrier_semaphore()
+    mesh_id = pl.DeviceIdType.MESH
+    for shift in range(1, frames):
+        pl.semaphore_signal(barrier, inc=1, device_id={"frame": lax.rem(me + shift, frames)},
+                            device_id_type=mesh_id)
+    pl.semaphore_signal(barrier, inc=1, device_id=across, device_id_type=mesh_id)
+    own = pltpu.make_async_copy(x_ref.at[me], mine_ref.at[me], own_sem)
+    own.start()
+    pl.semaphore_wait(barrier, frames)
+    copies = []
+    for shift in range(1, frames):
+        there = lax.rem(me + shift, frames)
+        copy = pltpu.make_async_remote_copy(
+            src_ref=x_ref.at[there], dst_ref=mine_ref.at[me], send_sem=send_sem.at[shift],
+            recv_sem=recv_sem.at[shift], device_id={"frame": there}, device_id_type=mesh_id)
+        copy.start()
+        copies.append(copy)
+
+    forwards = []
+    for shift in range(frames):
+        if shift:
+            copies[shift - 1].wait_recv()
+        else:
+            own.wait()
+        source = lax.rem(me - shift + frames, frames)
+        copy = pltpu.make_async_remote_copy(
+            src_ref=mine_ref.at[source], dst_ref=other_ref.at[source],
+            send_sem=fwd_send.at[shift], recv_sem=fwd_recv.at[shift], device_id=across,
+            device_id_type=mesh_id)
+        copy.start()
+        forwards.append(copy)
+    for copy in copies:
+        copy.wait_send()
+    for copy in forwards:
+        copy.wait()
+
+
+def return_heads(attn):
+    frames = attn.shape[0]
+    out = jax.ShapeDtypeStruct(attn.shape, attn.dtype)
+    return pl.pallas_call(
+        functools.partial(return_kernel, frames),
+        in_specs=[pl.BlockSpec(memory_space=pltpu.VMEM)],
+        out_specs=[pl.BlockSpec(memory_space=pltpu.VMEM)] * 2,
+        out_shape=[out, out],
+        scratch_shapes=[pltpu.SemaphoreType.DMA((frames,))] * 4 + [pltpu.SemaphoreType.DMA],
+        compiler_params=pltpu.CompilerParams(collective_id=2, has_side_effects=True),
+        name="return_heads",
+    )(attn)
+
+
 def gather_mp(block, size):
     if size != 2:
         return lax.all_gather(block, "mp", axis=block.ndim - 1, tiled=True)
@@ -103,10 +158,14 @@
     depth = w_qkv.shape[0]
     xin = jnp.where(token_mask[..., None] == 1, mask_embed, tokens)
     share = depth // dp_size
-    mine = lax.dynamic_slice_in_dim(
-        w_qkv.reshape(depth, 3 * heads_width), lax.axis_index("dp") * share, share, axis=0
-    )
-    weights = lax.all_gather(mine, ("frame", "dp"), axis=0, tiled=True)
+    start = lax.axis_index("dp") * share
+    weights = []
+    for part in range(3):
+        mine = lax.dynamic_slice(
+            w_qkv, (start, part, 0), (share, 1, heads_width)).reshape(share, heads_width)
+        if weights:
+            mine, _ = lax.optimization_barrier((mine, weights[-1][:1, :1]))
+        weights.append(lax.all_gather(mine, ("frame", "dp"), axis=0, tiled=True))
     if mp_size == 2:
         my_mp = lax.axis_index("mp")
         out_mine = lax.dynamic_slice_in_dim(w_out, my_mp * width, width, axis=1)
@@ -119,18 +178,25 @@
     frames = spread.shape[0] // clips
     local = spread.shape[1]
     features = gather_mp(spread.reshape(frames * clips * local, width), mp_size)
-    qkv = jnp.dot(features, weights, preferred_element_type=jnp.float32).astype(jnp.bfloat16)
-    attn = attend(qkv.reshape(frames, clips * local, 3 * heads_width), frames, heads_width)
-    back = lax.all_to_all(
-        attn.reshape(frames * clips, local, heads_width), "frame", split_axis=0, concat_axis=1,
-        tiled=True,
-    )
-    heads = back.reshape(clips * spots, heads_width)
+    query, keys, values = [
+        jnp.dot(features, w, preferred_element_type=jnp.float32)
+        .astype(jnp.bfloat16)
+        .reshape(frames, clips * local, heads_width)
+        for w in weights
+    ]
+    attn = attend(query, keys, values)
+    in_order = lambda blocks: (
+        blocks.reshape(frames, clips, local, heads_width)
+        .transpose(1, 0, 2, 3)
+        .reshape(clips * spots, heads_width)
+    )
     if mp_size == 2:
-        other_heads = lax.ppermute(heads, "mp", [(0, 1), (1, 0)])
+        heads, other_heads = [in_order(blocks) for blocks in return_heads(attn)]
         mixed_rows = jnp.dot(heads, out_mine, preferred_element_type=jnp.float32) + jnp.dot(
             other_heads, out_other, preferred_element_type=jnp.float32)
     else:
+        heads = in_order(
+            lax.all_to_all(attn, "frame", split_axis=0, concat_axis=0, tiled=True))
         out_block = lax.all_to_all(w_out, "mp", split_axis=1, concat_axis=0, tiled=True)
         mixed_rows = jnp.dot(gather_mp(heads, mp_size), out_block,
                              preferred_element_type=jnp.float32)

time: 442 us -> 516 us (1.17)
  waiting for transfers between devices: 279 us -> 349 us
  Pallas kernels: 22.9 us -> 58.8 us
  starting transfers between devices: 35.2 us -> 8.94 us
  local copies, waits for them, and re-layouts: 38 us -> 22.4 us
  matrix products: 35.5 us -> 42.2 us
    ppermute x1, waiting for transfers between devices: 28.1 us -> 137 us  [gather_mp(): other = lax.ppermute(block, 'mp', [(0, 1), (1, 0)])]
    pallas_call x0 -> x1, Pallas kernels: none -> 33.8 us  [return_heads(): pl.pallas_call(functools.partial(return_kernel, frames), in_specs=[pl.Blo...]
    all_to_all x1 -> x0, waiting for transfers between devices: 28.4 us -> none  [body(): lax.all_to_all(attn.reshape(frames * clips, local, heads_width), 'frame',...]
    all_to_all x1 -> x0, starting transfers between devices: 26 us -> none  [body(): lax.all_to_all(attn.reshape(frames * clips, local, heads_width), 'frame',...]
    ppermute x1 -> x0, waiting for transfers between devices: 15.6 us -> none  [body(): other_heads = lax.ppermute(heads, 'mp', [(0, 1), (1, 0)])]
    all_to_all x1, waiting for transfers between devices: 47.4 us -> 61.6 us  [body(): lax.all_to_all(xin.reshape(clips, spots, width), 'frame', split_axis=1, c...]
    dynamic_slice x2 -> x0, local copies, waits for them, and re-layouts: 11.9 us -> none  [body(): lax.dynamic_slice_in_dim(w_qkv.reshape(depth, 3 * heads_width), lax.axis_...]
    all_gather x1 -> x3, waiting for transfers between devices: 159 us -> 148 us  [body(): weights.append(lax.all_gather(mine, ('frame', 'dp'), axis=0, tiled=True))]
  transfers between devices with their start and end apart: 6 -> 6, of which waited for: 5 -> 4; matrix products, arithmetic and copies ran while one was open for 11% -> 11% of each run, Pallas kernels for 2% -> 8%
where the time goes in v3:
time: 516 us; the launch traced here: 515 us
  waiting for transfers between devices  349 us (68%)
  Pallas kernels  58.8 us (11%)
  matrix products  42.2 us (8%)
  local copies, waits for them, and re-layouts  22.4 us (4%)
  other arithmetic  20.3 us (4%)
  between operations  14 us (3%)
  starting transfers between devices  8.94 us (2%)
    all_gather x3, waiting for transfers between devices, body(): weights.append(lax.all_gather(mine, ('frame', 'dp'), axis=0, tiled=True))  148 us
    ppermute x1, waiting for transfers between devices, gather_mp(): other = lax.ppermute(block, 'mp', [(0, 1), (1, 0)])  137 us
    all_to_all x1, waiting for transfers between devices, body(): lax.all_to_all(xin.reshape(clips, spots, width), 'frame', split_axis=1, c...  61.6 us
    pallas_call x1, Pallas kernels, return_heads(): pl.pallas_call(functools.partial(return_kernel, frames), in_specs=[pl.Blo...  33.8 us
    dot_general x3, matrix products, body(): jnp.dot(features, w, preferred_element_type=jnp.float32)  30.1 us
    pallas_call x1, Pallas kernels, spread_terms(): pl.pallas_call(functools.partial(spread_kernel, frames, dps), in_specs=[p...  15.6 us
    convert_element_type x1, other arithmetic, body(): (xin.astype(jnp.float32) + gate[:, None, None, :] * mixed).astype(jnp.bfl...  12.7 us
  transfers between devices with their start and end apart: 6, of which 4 were waited for; matrix products, arithmetic and copies ran while one was open for 11% of the time, Pallas kernels for 8%

profile of v3, /device:TPU:1, one launch (start us, length us, event | category | flops | bytes accessed | tf_op | source)
XLA Modules:
  0.0 515.4 jit_solution(18247672027489534932)
XLA Ops:
  7.2 0.0 copy-start
  7.2 0.0 all-gather.7.cloned.1.call-start
  7.2 0.0 copy-start.9
  7.2 0.0 copy-start.4
  7.3 0.0 copy-start.8
  7.3 3.6 dynamic-slice_bitcast_fusion
  10.8 0.0 all-gather.7.cloned.1.call-update
  10.9 0.0 all-gather.9.cloned.1.call-start
  10.9 0.7 all-gather.9.cloned.1.call-update
  11.6 0.0 all-gather.5.cloned.1.call-start
  11.6 0.7 all-gather.5.cloned.1.call-update
  12.3 0.0 copy-done.9
  12.4 0.1 copy.31
  12.5 0.0 copy-done.4
  12.5 0.0 copy-done.8
  12.5 3.2 fusion.11
  15.7 6.4 %all-to-all-start = ((bf16[2,160,2560]{2,0,1:T(2,128)(2,1)}), bf16[2,160,2560]{2,0,1:T(2,128)(2,1)S(1)}, u32[]{:S(2)}, u32[]{:S(2)}) async-start(bf16[2,160,2560]{2,0,1:T(2,128)(2,1)} %fusion.11), calls=%async_computation | async-start | bytes 3276800 | tf_op jit(solution)/shard_map/all_to_all | solution.py:175
  22.1 7.2 %constant_dynamic-slice_fusion = bf16[1536,2560]{1,0:T(8,128)(2,1)} fusion(bf16[1536,5120]{1,0:T(8,128)(2,1)} %param.13, s32[]{:T(128)S(6)} %select_n.33), kind=kLoop, calls=%fused_computation.26 | loop fusion | bytes 15728644 | tf_op jit(solution)/shard_map/dynamic_slice | solution.py:173
  29.3 1.2 collective-permute-start.1
  30.6 61.6 %all-to-all-done = bf16[2,160,2560]{2,0,1:T(2,128)(2,1)S(1)} async-done(((bf16[2,160,2560]{2,0,1:T(2,128)(2,1)}), bf16[2,160,2560]{2,0,1:T(2,128)(2,1)S(1)}, u32[]{:S(2)}, u32[]{:S(2)}) %all-to-all-start) | async-done | bytes 1638432 | tf_op jit(solution)/shard_map/all_to_all | solution.py:175
  92.2 0.0 copy-start.3
  92.2 1.2 copy-done.3
  93.4 0.0 copy-start.10
  93.4 1.7 copy.23
  95.1 1.3 reshape.77
  96.4 1.2 collective-permute-start
  97.6 0.0 copy-done.10
  97.6 0.0 copy-done.11
  97.6 0.2 fusion.14
  97.8 0.0 copy-done
  97.8 0.3 fusion.22
  98.1 137.4 %collective-permute-done = bf16[320,2560]{1,0:T(8,128)(2,1)} collective-permute-done((bf16[320,2560]{1,0:T(8,128)(2,1)}, bf16[320,2560]{1,0:T(8,128)(2,1)}, u32[]{:S(2)}, u32[]{:S(2)}) %collective-permute-start) | collective-permute-done | bytes 1638432 | tf_op jit(solution)/shard_map/ppermute | solution.py:147
  235.5 3.3 broadcast_select_fusion.2
  238.8 10.1 %convolution_convert_fusion = bf16[320,1536]{1,0:T(8,128)(2,1)} fusion(bf16[5120,1536]{1,0:T(8,128)(2,1)} %all-gather.7.cloned.1.call-done, bf16[320,2560]{1,0:T(8,128)(2,1)} %get-tuple-element.12, bf16[320,2560]{1,0:T(8,128)(2,1)S(1)} %get-tuple-element.11), kind=kOutput, calls=%fused_computation.12 | convolution fusion | flops 5040209920 | bytes 19988480 | tf_op jit(solution)/shard_map/dot_general | solution.py:182
  248.9 38.0 %all-gather.9.cloned.1.call-done = bf16[5120,1,1536]{2,0,1:T(8,128)(2,1)} async-done(((bf16[320,1,1536]{2,0,1:T(8,128)(2,1)}), bf16[5120,1,1536]{2,0,1:T(8,128)(2,1)}) %all-gather.9.cloned.1.call-update) | async-done | bytes 15728656 | tf_op jit(solution)/shard_map/all_gather | solution.py:168
  286.9 10.1 %fusion.6 = bf16[320,1536]{1,0:T(8,128)(2,1)} fusion(bf16[5120,1,1536]{2,0,1:T(8,128)(2,1)} %all-gather.9.cloned.1.call-done, bf16[320,2560]{1,0:T(8,128)(2,1)} %get-tuple-element.12, bf16[320,2560]{1,0:T(8,128)(2,1)S(1)} %get-tuple-element.11), kind=kOutput, calls=%fused_computation.11 | convolution fusion | flops 5040209920 | bytes 19988480 | tf_op jit(solution)/shard_map/dot_general | solution.py:182
  297.0 110.4 %all-gather.5.cloned.1.call-done = bf16[5120,1536]{1,0:T(8,128)(2,1)} async-done(((bf16[320,1536]{1,0:T(8,128)(2,1)}), bf16[5120,1536]{1,0:T(8,128)(2,1)}) %all-gather.5.cloned.1.call-update) | async-done | bytes 15728656 | tf_op jit(solution)/shard_map/all_gather | solution.py:168
  407.4 9.9 %convolution_convert_fusion.1 = bf16[320,1536]{1,0:T(8,128)(2,1)} fusion(bf16[5120,1536]{1,0:T(8,128)(2,1)} %all-gather.5.cloned.1.call-done, bf16[320,2560]{1,0:T(8,128)(2,1)} %get-tuple-element.12, bf16[320,2560]{1,0:T(8,128)(2,1)S(1)} %get-tuple-element.11), kind=kOutput, calls=%fused_computation.13 | convolution fusion | flops 5040209920 | bytes 19988480 | tf_op jit(solution)/shard_map/dot_general | solution.py:182
  417.3 9.5 %attend.1.x_ref = bf16[8,40,1536]{2,1,0:T(8,128)(2,1)} custom-call(bf16[8,40,1536]{2,1,0:T(8,128)(2,1)} %bitcast.42, bf16[8,40,1536]{2,1,0:T(8,128)(2,1)} %bitcast.43, bf16[8,40,1536]{2,1,0:T(8,128)(2,1)} %bitcast.41), custom_call_target="tpu_custom_call" | custom-call | flops 15728640 | bytes 3932160 | tf_op jit(solution)/shard_map/attend/pallas_call | solution.py:34
  426.8 33.8 %return_heads.1 = (bf16[8,40,1536]{2,1,0:T(8,128)(2,1)}, bf16[8,40,1536]{2,1,0:T(8,128)(2,1)}) custom-call(bf16[8,40,1536]{2,1,0:T(8,128)(2,1)} %attend.1.x_ref), custom_call_target="tpu_custom_call" | custom-call | tf_op jit(solution)/shard_map/return_heads/pallas_call | solution.py:133
  460.6 0.0 copy-start.7
  460.6 1.6 copy.24
  462.1 0.3 copy.25
  462.5 0.3 reshape.85
  462.7 0.0 copy-done.7
  462.7 0.3 copy.26
  463.0 0.3 copy.27
  463.3 0.3 reshape.87
  463.6 5.0 fusion.2
  468.6 0.0 copy-start.6
  468.6 0.0 collective-permute-done.1
  468.6 5.4 %convolution_add_fusion = f32[320,2560]{1,0:T(8,128)S(1)} fusion(f32[320,2560]{1,0:T(8,128)S(1)} %fusion.2, bf16[320,1536]{1,0:T(8,128)(2,1)S(1)} %reshape.87, bf16[1536,2560]{1,0:T(8,128)(2,1)} %collective-permute-done.1), kind=kOutput, calls=%fused_computation.4 | convolution fusion | flops 2517401600 | bytes 15400960 | tf_op jit(solution)/shard_map/dot_general | solution.py:195
  474.0 0.0 copy-start.2
  474.0 1.7 copy-done.2
  475.7 0.0 copy-done.6
  475.7 0.4 multiply_reduce_fusion
  476.1 0.6 fusion.12.x_ref
  476.8 15.6 %spread_terms.1 = f32[16,2,2688]{2,1,0:T(2,128)} custom-call(f32[2,2688]{1,0:T(2,128)} %fusion.12.x_ref), custom_call_target="tpu_custom_call" | custom-call | tf_op jit(solution)/shard_map/spread_terms/pallas_call | solution.py:77
  492.4 1.2 reshape.89
  493.6 1.2 fusion.9
  494.8 0.0 copy-done.5
  494.8 12.7 %fusion.5 = bf16[2,1,160,2560]{3,0,2,1:T(2,128)(2,1)S(1)} fusion(f32[2,1,160,2560]{3,2,0,1:T(8,128)} %bitcast.37, f32[2,2560]{1,0:T(2,128)S(1)} %fusion.22, bf16[2,1,160,2560]{3,2,1,0:T(8,128)(2,1)S(1)} %copy-done.5, bf16[2560]{0:T(1024)(128)(2,1)S(1)} %copy-done.8, pred[2,160]{0,1:T(8,128)(4,1)S(1)} %bitcast.45), kind=kLoop, calls=%fused_computation.8 | loop fusion | flops 4096000 | bytes 6579520 | tf_op jit(solution)/shard_map/convert_element_type | solution.py:209
  507.5 1.3 copy.30
  508.8 0.0 copy-done.1
  (5 shorter events, 0.0 us)
Async XLA Ops:
  7.2 90.7 %copy-start = (f32[32,2560]{1,0:T(8,128)S(1)}, f32[32,2560]{1,0:T(8,128)}, u32[]{:S(2)}) copy-start(f32[32,2560]{1,0:T(8,128)} %param.16) | copy-start | bytes 983044
  7.2 231.6 %all-gather.7.cloned.1.call-start = ((), (), s32[]{:S(2)}) async-start(), calls=%async_computation.2 | async-start | bytes 16711680 | tf_op jit(solution)/shard_map/all_gather | solution.py:168
  7.2 5.1 copy-start.9
  7.2 5.3 %copy-start.4 = (bf16[2,1,160,2560]{3,2,1,0:T(8,128)(2,1)S(1)}, bf16[2,1,160,2560]{3,2,1,0:T(8,128)(2,1)}, u32[]{:S(2)}) copy-start(bf16[2,1,160,2560]{3,2,1,0:T(8,128)(2,1)} %param.9) | copy-start | bytes 4915204
  7.3 5.3 %copy-start.8 = (bf16[2560]{0:T(1024)(128)(2,1)S(1)}, bf16[2560]{0:T(1024)(128)(2,1)}, u32[]{:S(2)}) copy-start(bf16[2560]{0:T(1024)(128)(2,1)} %param.11) | copy-start | bytes 15364
  10.9 276.1 %all-gather.9.cloned.1.call-start = ((), (), s32[]{:S(2)}) async-start(), calls=%async_computation.3 | async-start | bytes 16711680 | tf_op jit(solution)/shard_map/all_gather | solution.py:168
  11.6 395.8 %all-gather.5.cloned.1.call-start = ((), (), s32[]{:S(2)}) async-start(), calls=%async_computation.1 | async-start | bytes 16711680 | tf_op jit(solution)/shard_map/all_gather | solution.py:168
  15.7 76.5 %all-to-all-start = ((bf16[2,160,2560]{2,0,1:T(2,128)(2,1)}), bf16[2,160,2560]{2,0,1:T(2,128)(2,1)S(1)}, u32[]{:S(2)}, u32[]{:S(2)}) async-start(bf16[2,160,2560]{2,0,1:T(2,128)(2,1)} %fusion.11), calls=%async_computation | async-start | bytes 3276800 | tf_op jit(solution)/shard_map/all_to_all | solution.py:175
  29.3 439.3 %collective-permute-start.1 = (bf16[1536,2560]{1,0:T(8,128)(2,1)}, bf16[1536,2560]{1,0:T(8,128)(2,1)}, u32[]{:S(2)}, u32[]{:S(2)}) collective-permute-start(bf16[1536,2560]{1,0:T(8,128)(2,1)} %constant_dynamic-slice_fusion), channel_id=1, source_target_pairs={{0,2},{2,0},{1,3},{3,1},{4,6},{6,4},{5,7},{7,5},{8,10},{10,8},{9,1... | collective-permute-start | bytes 23592968 | tf_op jit(solution)/shard_map/ppermute | solution.py:172
  92.2 1.2 copy-start.3
  93.4 4.3 copy-start.10
  93.4 4.3 copy-start.11
  96.4 139.1 %collective-permute-start = (bf16[320,2560]{1,0:T(8,128)(2,1)}, bf16[320,2560]{1,0:T(8,128)(2,1)}, u32[]{:S(2)}, u32[]{:S(2)}) collective-permute-start(bf16[320,2560]{1,0:T(8,128)(2,1)} %reshape.77), channel_id=1, source_target_pairs={{0,2},{2,0},{1,3},{3,1},{4,6},{6,4},{5,7},{7,5},{8,10},{10,8},{9,1... | collective-permute-start | bytes 4915208 | tf_op jit(solution)/shard_map/ppermute | solution.py:147
  460.6 2.2 copy-start.7
  468.6 7.1 %copy-start.6 = (bf16[2,1,160,2560]{3,2,1,0:T(8,128)(2,1)S(1)}, bf16[2,1,160,2560]{3,2,1,0:T(8,128)(2,1)}, u32[]{:S(2)}) copy-start(bf16[2,1,160,2560]{3,2,1,0:T(8,128)(2,1)} %param.17) | copy-start | bytes 4915204
  474.0 1.7 copy-start.2
  475.7 19.1 %copy-start.5 = (bf16[2,1,160,2560]{3,2,1,0:T(8,128)(2,1)S(1)}, bf16[2,1,160,2560]{3,2,1,0:T(8,128)(2,1)}, u32[]{:S(2)}) copy-start(bf16[2,1,160,2560]{3,2,1,0:T(8,128)(2,1)} %param.9) | copy-start | bytes 4915204
  494.8 14.1 %copy-start.1 = (f32[32,2560]{1,0:T(8,128)S(1)}, f32[32,2560]{1,0:T(8,128)}, u32[]{:S(2)}) copy-start(f32[32,2560]{1,0:T(8,128)} %param.16) | copy-start | bytes 983044
Sparse Core Ops, SparseCore 0:
  11.0 155.6 all-gather.6
  169.0 117.9 all-gather.8
  289.2 118.1 all-gather.4
